TPU v7x, 32 devices: a whole 2x2x4 slice. The times are simulated.
32 devices in a mesh: grp: 2 (over y), tp: 8 (over z, x), sub: 2 (over core).
Axes of the slice: x: 2, y: 2, z: 4, core: 2. Of those that a mesh axis runs over, the one named last changes fastest.
Arguments:
- hidden_in: bfloat16 [32, 2, 4096], P('grp', 'sub', 'tp'), parts along dimension 0, may hold values from -16 to 16
- norm_attn: float32 [8192], replicated, may hold values from 0.25 to 1.75
- w_query: bfloat16 [8192, 2, 4096], P(None, 'sub', 'tp'), may hold values from -0.0625 to 0.0625
- w_key: bfloat16 [8192, 2, 512], P(None, 'sub', 'tp'), may hold values from -0.0625 to 0.0625
- w_value: bfloat16 [8192, 2, 512], P(None, 'sub', 'tp'), may hold values from -0.0625 to 0.0625
- w_out: bfloat16 [2, 4096, 2, 4096], P('sub', None, None, 'tp'), may hold values from -0.0625 to 0.0625
- norm_ffn: float32 [8192], replicated, may hold values from 0.25 to 1.75
- w_gate: bfloat16 [2, 4096, 14336], P('sub', None, 'tp'), may hold values from -0.0625 to 0.0625
- w_up: bfloat16 [2, 4096, 14336], P('sub', None, 'tp'), may hold values from -0.0625 to 0.0625
- w_down: bfloat16 [14336, 2, 4096], P('tp', 'sub'), may hold values from -0.0625 to 0.0625
- cache_keys: bfloat16 [32, 64, 8, 128], P('grp', 'tp', 'sub'), parts along dimension 0, may hold values from -250 to 250
- cache_values: bfloat16 [32, 64, 8, 128], P('grp', 'tp', 'sub'), parts along dimension 0, may hold values from -6 to 6
- lengths: int32 [32], P('grp'), parts along dimension 0, may hold values from 1 to 64, as said below
Outputs:
- hidden_out: bfloat16 [32, 2, 4096], P('grp', 'sub', 'tp'), parts along dimension 0
There are 2 independent parts, one for each index of `grp`. A program takes and returns all parts, laid end to end along the dimension named above; an argument that names none is the same for every part. Nothing has to cross between parts.
Inputs may be any that keep to these rules, and one draw needn't show every extreme that they name: `lengths`: some sequence has 64 live positions and some has 1.
All inputs are finite; a program needn't handle non-finite values.
Results may differ from a plain program's by a relative error of at most 0.012.
The roundings to bfloat16 on the way count: a program that leaves them out, or rounds other values in their place, can miss the bound.
Values may be sent and summed in bfloat16 or wider, within the bound.
A program may use at most 128 MiB of HBM per device.

v0:
```python
import math
import jax
import jax.numpy as jnp
from jax import lax
from jax.sharding import PartitionSpec as P

HD = 128
epsilon = 1e-05
rope_base = 500000.0
floor_score = -1e30


def joined(part, axis, combine):
    gathered = jax.tree.map(lambda a: lax.all_gather(a, axis), part)

    def take(source):
        return jax.tree.map(lambda a: lax.dynamic_index_in_dim(a, source, 0, False), gathered)

    return lax.fori_loop(
        1, lax.axis_size(axis), lambda source, state: combine(state, take(source)), take(0)
    )


def rope_angles(lengths):
    frequencies = rope_base ** (-(jnp.arange(HD // 2, dtype=jnp.float32) * 2.0) / HD)
    return lengths.astype(jnp.float32)[:, None] * frequencies[None, :]


def rotate(vectors, angles):
    middle_index = vectors.shape[-1] // 2
    cosine = jnp.cos(angles)[:, None, :]
    sine = jnp.sin(angles)[:, None, :]
    lower = vectors[..., :middle_index]
    upper = vectors[..., middle_index:]
    return jnp.concatenate([lower * cosine - upper * sine, upper * cosine + lower * sine], axis=-1)


def spread_rows(shard):
    across = lax.all_gather(shard, "tp", axis=2, tiled=True)
    return lax.all_gather(across, "sub", axis=1, tiled=True)


def half_rows_of(shard):
    return lax.all_gather(shard, "tp", axis=2, tiled=True)


def join_partials(earlier, later):
    earlier_max, earlier_sum, earlier_out = earlier
    later_max, later_sum, later_out = later
    highest = jnp.maximum(earlier_max, later_max)
    earlier_scale = jnp.exp(earlier_max - highest)
    later_scale = jnp.exp(later_max - highest)
    joined_sum = earlier_sum * earlier_scale + later_sum * later_scale
    joined_out = earlier_out * earlier_scale[..., None] + later_out * later_scale[..., None]
    return (highest, joined_sum, joined_out)


def per_device(
    hidden_in,
    norm_attn,
    w_query,
    w_key,
    w_value,
    w_out,
    norm_ffn,
    w_gate,
    w_up,
    w_down,
    cache_keys,
    cache_values,
    lengths,
):
    seq_count = hidden_in.shape[0]
    shard_width = hidden_in.shape[2]
    half_width = shard_width * lax.axis_size("tp")
    model_width = half_width * lax.axis_size("sub")
    tp_pos = lax.axis_index("tp")
    sub_pos = lax.axis_index("sub")
    residual = hidden_in.astype(jnp.float32)
    whole_rows = spread_rows(hidden_in).astype(jnp.float32)
    factor = lax.rsqrt(jnp.mean(whole_rows * whole_rows, axis=(1, 2)) + epsilon)
    gain_whole = norm_attn.reshape(whole_rows.shape[1], half_width)
    gathered = (whole_rows * factor[:, None, None] * gain_whole).astype(jnp.bfloat16)
    flattened = gathered.reshape(seq_count, model_width)
    query_part = jnp.dot(
        flattened, w_query.reshape(model_width, -1), preferred_element_type=jnp.float32
    ).astype(jnp.bfloat16)
    key_part = jnp.dot(
        flattened, w_key.reshape(model_width, -1), preferred_element_type=jnp.float32
    ).astype(jnp.bfloat16)
    value_part = jnp.dot(
        flattened, w_value.reshape(model_width, -1), preferred_element_type=jnp.float32
    ).astype(jnp.bfloat16)
    query, key_new, value_new = (
        lax.all_gather(query_part, "tp", axis=1, tiled=True),
        lax.all_gather(key_part, "tp", axis=1, tiled=True),
        lax.all_gather(value_part, "tp", axis=1, tiled=True),
    )
    query_heads = query.shape[1] // HD
    kv_heads = key_new.shape[1] // HD
    group_size = query_heads // kv_heads
    angles = rope_angles(lengths)
    query_rot = rotate(
        query.astype(jnp.float32).reshape(seq_count, query_heads, HD), angles
    ).astype(jnp.bfloat16)
    key_rot = rotate(key_new.astype(jnp.float32).reshape(seq_count, kv_heads, HD), angles).astype(
        jnp.bfloat16
    )
    grouped = query_rot.reshape(seq_count, kv_heads, group_size, HD)
    values_new = value_new.astype(jnp.float32).reshape(seq_count, kv_heads, 1, HD)
    span = cache_keys.shape[1]
    scores = jnp.einsum(
        "bkgd,blkd->bkgl", grouped, cache_keys, preferred_element_type=jnp.float32
    ) / math.sqrt(HD)
    places = tp_pos * span + jnp.arange(span, dtype=jnp.int32)
    live = (places[None, :] < lengths[:, None])[:, None, None, :]
    masked = jnp.where(live, scores, floor_score)
    local_max = jnp.max(masked, axis=-1)
    weights = jnp.where(live, jnp.exp(masked - local_max[..., None]), 0.0)
    local_sum = jnp.sum(weights, axis=-1)
    local_out = jnp.einsum(
        "bkgl,blkd->bkgd",
        weights,
        cache_values.astype(jnp.float32),
        precision=lax.Precision.HIGHEST,
    )
    own_score = jnp.sum(
        grouped.astype(jnp.float32) * key_rot.astype(jnp.float32)[:, :, None, :], axis=-1
    ) / math.sqrt(HD)
    joined_max, joined_sum, joined_out = joined(
        (local_max, local_sum, local_out), "tp", join_partials
    )
    highest = jnp.maximum(joined_max, own_score)
    kept_scale = jnp.exp(joined_max - highest)
    own_weight = jnp.exp(own_score - highest)
    numerator = joined_out * kept_scale[..., None] + own_weight[..., None] * values_new
    denominator = joined_sum * kept_scale + own_weight
    attended = (numerator / denominator[..., None]).reshape(seq_count, -1).astype(jnp.bfloat16)
    out_part = jnp.dot(
        attended, w_out.reshape(attended.shape[1], -1), preferred_element_type=jnp.float32
    )
    out_part = out_part.reshape(seq_count, -1, shard_width)
    mixed = lax.psum_scatter(out_part, "sub", scatter_dimension=1, tiled=True)
    middle = (residual + mixed).astype(jnp.bfloat16)
    middle_float = middle.astype(jnp.float32)
    raw_half = half_rows_of(middle).astype(jnp.float32)
    partial_squares = jnp.sum(raw_half * raw_half, axis=(1, 2))
    squares_mid = lax.psum(partial_squares, "sub")
    factor_mid = lax.rsqrt(squares_mid / model_width + epsilon)
    gain_half = lax.dynamic_slice_in_dim(norm_ffn, sub_pos * half_width, half_width)
    half_rows = (raw_half * factor_mid[:, None, None] * gain_half).astype(jnp.bfloat16)
    half_flat = half_rows.reshape(seq_count, half_width)
    gate_part = jnp.dot(
        half_flat, w_gate.reshape(half_width, -1), preferred_element_type=jnp.float32
    )
    up_part = jnp.dot(half_flat, w_up.reshape(half_width, -1), preferred_element_type=jnp.float32)
    gate_total, up_total = lax.psum((gate_part, up_part), "sub")
    hidden = (jax.nn.silu(gate_total) * up_total).astype(jnp.bfloat16)
    down_part = jnp.dot(
        hidden, w_down.reshape(hidden.shape[1], -1), preferred_element_type=jnp.float32
    )
    down_total = lax.psum(down_part, "tp")
    down_share = lax.dynamic_slice_in_dim(down_total, tp_pos * shard_width, shard_width, 1)
    return (middle_float + down_share[:, None, :]).astype(jnp.bfloat16)


def solution(mesh):
    in_specs = (
        P("grp", "sub", "tp"),
        P(),
        P(None, "sub", "tp"),
        P(None, "sub", "tp"),
        P(None, "sub", "tp"),
        P("sub", None, None, "tp"),
        P(),
        P("sub", None, "tp"),
        P("sub", None, "tp"),
        P("tp", "sub", None),
        P("grp", "tp", "sub", None),
        P("grp", "tp", "sub", None),
        P("grp"),
    )
    out_specs = P("grp", "sub", "tp")
    return jax.shard_map(
        per_device, mesh=mesh, in_specs=in_specs, out_specs=out_specs, check_vma=False
    )
```

profile of v0, /device:TPU:0, one launch (start us, length us, event | category | flops | bytes accessed | tf_op | source)
XLA Modules:
  0.0 410.7 jit_solution(6426538400944346462)
XLA Ops:
  6.6 32.7 %all_gather.36 = bf16[16,1,4096]{2,0,1:T(8,128)(2,1)S(1)} all-gather(bf16[16,1,512]{2,0,1:T(8,128)(2,1)} %param.15), channel_id=1, replica_groups=mesh['grp'=2,'tp'=8,'sub'=2] {'tp'}, dimensions={2}, use_global_device_ids=true | all-gather | bytes 147456 | tf_op jit(solution)/shard_map/all_gather | solution.py:39
  39.3 2.0 all_gather.37
  42.4 4.6 %fusion.12 = bf16[16,512]{1,0:T(8,128)(2,1)S(1)} fusion(bf16[16,8192]{1,0:T(8,128)(2,1)S(1)} %bitcast.90, bf16[8192,1,512]{2,0,1:T(8,128)(2,1)} %param.17), kind=kOutput, calls=%fused_computation.18 | convolution fusion | flops 134225920 | bytes 8667136 | tf_op jit(solution)/shard_map/dot_general | solution.py:85
  47.0 30.5 %all_gather.38 = bf16[16,4096]{1,0:T(8,128)(2,1)S(1)} all-gather(bf16[16,512]{1,0:T(8,128)(2,1)S(1)} %fusion.12), channel_id=1, replica_groups=mesh['grp'=2,'tp'=8,'sub'=2] {'tp'}, dimensions={1}, use_global_device_ids=true | all-gather | bytes 147456 | tf_op jit(solution)/shard_map/all_gather | solution.py:95
  78.3 1.3 fusion.26
  79.9 31.0 %all-gather.1 = f32[128,4,8]{2,1,0:T(4,128)S(1)} all-gather(f32[16,4,8]{2,1,0:T(4,128)S(1)} %fusion.27), channel_id=3, replica_groups=mesh['grp'=2,'tp'=8,'sub'=2] {'tp'}, dimensions={0}, use_global_device_ids=true | all-gather | bytes 18432 | tf_op jit(solution)/shard_map/all_gather | solution.py:14
  111.1 31.7 %all-gather = f32[128,4,8]{2,1,0:T(4,128)S(1)} all-gather(f32[16,4,8]{2,1,0:T(4,128)S(1)} %get-tuple-element.236), channel_id=2, replica_groups=mesh['grp'=2,'tp'=8,'sub'=2] {'tp'}, dimensions={0}, use_global_device_ids=true | all-gather | bytes 18432 | tf_op jit(solution)/shard_map/all_gather | solution.py:14
  143.4 30.6 %all-gather.3 = bf16[8,64,16]{1,2,0:T(8,128)(2,1)S(1)} all-gather(bf16[1,64,16]{1,2,0:T(8,128)(2,1)S(1)} %fusion.15), channel_id=1, replica_groups=mesh['grp'=2,'tp'=8,'sub'=2] {'tp'}, dimensions={0}, use_global_device_ids=true | all-gather | bytes 18432 | tf_op jit(solution)/shard_map/all_gather | solution.py:96
  175.1 30.6 %all-gather.4 = bf16[8,64,16]{1,2,0:T(8,128)(2,1)S(1)} all-gather(bf16[1,64,16]{1,2,0:T(8,128)(2,1)S(1)} %fusion.16), channel_id=1, replica_groups=mesh['grp'=2,'tp'=8,'sub'=2] {'tp'}, dimensions={0}, use_global_device_ids=true | all-gather | bytes 18432 | tf_op jit(solution)/shard_map/all_gather | solution.py:97
  205.8 9.3 %copy.83 = bf16[512,8,2,512]{3,1,2,0:T(8,128)(2,1)} copy(bf16[512,8,2,512]{3,2,1,0:T(2,128)(2,1)} %bitcast.89) | data formatting | bytes 16777216
  215.1 11.4 %copy.75 = bf16[1024,4096]{1,0:T(8,128)(2,1)} copy(bf16[1024,4096]{0,1:T(8,128)(2,1)} %bitcast.88) | data formatting | bytes 16777216 | tf_op jit(solution)/shard_map/dot_general | solution.py:139
  227.5 10.0 %while.19 = (s32[]{:T(128)}, f32[16,4,8]{0,2,1:T(8,128)S(1)}, f32[16,4,8]{0,2,1:T(8,128)S(1)}, f32[16,4,8,128]{3,2,1,0:T(8,128)S(1)}, f32[8,16,4,8]{1,3,2,0:T(8,...) while((s32[]{:T(128)}, f32[16,4,8]{0,2,1:T(8,128)S(1)}, ...), condition=%wide.region_4.5_spmd, body=%wide.region_3.4_spmd.sunk | while | flops 199685 | bytes 815255 | solution.py:19
  227.7 1.2 fusion.58
  231.9 1.2 fusion.58
  238.1 6.3 %fusion.49 = f32[16,2,512]{2,0,1:T(8,128)} fusion(bf16[16,4096,1]{1,0,2:T(8,128)(2,1)S(1)} %reshape.198, bf16[2,512,4096]{2,1,0:T(8,128)(2,1)} %bitcast.87), kind=kOutput, calls=%fused_computation.77 | convolution fusion | flops 134217728 | bytes 8585216 | tf_op jit(solution)/shard_map/dot_general | solution.py:139
  244.5 8.5 %reduce-scatter.2.cloned.1.call-done = f32[16,1,512]{2,0,1:T(8,128)} async-done(((f32[16,2,512]{2,0,1:T(8,128)}), f32[16,1,512]{2,0,1:T(8,128)}) %reduce-scatter.2.cloned.1.call-update) | async-done | bytes 32784 | tf_op jit(solution)/shard_map/reduce_scatter | solution.py:143
  253.8 30.8 %all_gather.47 = bf16[16,1,4096]{2,0,1:T(8,128)(2,1)S(1)} all-gather(bf16[16,1,512]{2,0,1:T(8,128)(2,1)S(1)} %add_convert_fusion.1), channel_id=1, replica_groups=mesh['grp'=2,'tp'=8,'sub'=2] {'tp'}, dimensions={2}, use_global_device_ids=true | all-gather | bytes 147456 | tf_op jit(solution)/shard_map/all_gather | solution.py:44
  284.7 2.6 psum.28
  287.3 7.9 %fusion.7 = f32[16,1792]{1,0:T(8,128)} fusion(bf16[1,4096,1792]{2,1,0:T(8,128)(2,1)} %param.22, bf16[16,1,4096]{2,0,1:T(8,128)(2,1)S(1)} %all_gather.47, f32[4096]{0:T(1024)S(1)} %dynamic_slice.50, f32[16]{0:T(128)S(1)} %add_rsqrt_fusion), kind=kOutput, calls=%fused_computation.12 | convolution fusion | flops 235143168 | bytes 14942272 | tf_op jit(solution)/shard_map/dot_general | solution.py:153
  295.2 7.9 %fusion.5 = f32[16,1792]{1,0:T(8,128)} fusion(bf16[1,4096,1792]{2,1,0:T(8,128)(2,1)} %param.23, bf16[16,1,4096]{2,0,1:T(8,128)(2,1)S(1)} %all_gather.47, f32[4096]{0:T(1024)S(1)} %dynamic_slice.50, f32[16]{0:T(128)S(1)} %add_rsqrt_fusion), kind=kOutput, calls=%fused_computation.10 | convolution fusion | flops 235143168 | bytes 14942272 | tf_op jit(solution)/shard_map/dot_general | solution.py:156
  303.2 19.1 %all-reduce.6.cloned.1.call-done = (f32[16,1792]{1,0:T(8,128)}, f32[16,1792]{1,0:T(8,128)}) async-done(((f32[16,1792]{1,0:T(8,128)}, f32[16,1792]{1,0:T(8,128)}), (f32[16,1792]{1,0:T(8,128)}, f32[16,1792]{1,0:T(8,128)})) %all-reduce.6.cloned.1.call-update) | async-done | bytes 229392 | tf_op jit(solution)/shard_map/psum | solution.py:157
  322.4 8.0 %fusion.3 = f32[16,4096]{1,0:T(8,128)} fusion(bf16[1792,1,4096]{2,0,1:T(8,128)(2,1)} %param.24, f32[16,1792]{1,0:T(8,128)} %get-tuple-element.221, f32[16,1792]{1,0:T(8,128)} %get-tuple-element.222), kind=kOutput, calls=%fused_computation.8 | convolution fusion | flops 235053056 | bytes 15171584 | tf_op jit(solution)/shard_map/dot_general | solution.py:159
  330.4 72.4 %all-reduce.4.cloned.1.call-done = f32[16,4096]{1,0:T(8,128)} async-done(((f32[16,4096]{1,0:T(8,128)}), f32[16,4096]{1,0:T(8,128)}) %all-reduce.4.cloned.1.call-update) | async-done | bytes 262160 | tf_op jit(solution)/shard_map/psum | solution.py:162
  402.8 1.4 fusion.37
  (95 shorter events, 14.0 us)
Async XLA Ops:
  6.5 136.5 %copy-start = (bf16[8192,1,64]{0,2,1:T(8,128)(2,1)S(1)}, bf16[8192,1,64]{0,2,1:T(8,128)(2,1)}, u32[]{:S(2)}) copy-start(bf16[8192,1,64]{0,2,1:T(8,128)(2,1)} %param.18) | copy-start | bytes 3145732
  6.5 71.1 %copy-start.7 = (s32[16]{0:T(128)S(1)}, s32[16]{0:T(128)}, u32[]{:S(2)}) copy-start(s32[16]{0:T(128)} %param.27) | copy-start | bytes 196
  6.5 71.4 %copy-start.3 = (bf16[16,8,4,128]{3,2,1,0:T(4,128)(2,1)S(1)}, bf16[16,8,4,128]{3,2,1,0:T(4,128)(2,1)}, u32[]{:S(2)}) copy-start(bf16[16,8,4,128]{3,2,1,0:T(4,128)(2,1)} %param.25) | copy-start | bytes 393220
  6.5 71.8 %copy-start.4 = (bf16[16,8,4,128]{3,2,1,0:T(4,128)(2,1)S(1)}, bf16[16,8,4,128]{3,2,1,0:T(4,128)(2,1)}, u32[]{:S(2)}) copy-start(bf16[16,8,4,128]{3,2,1,0:T(4,128)(2,1)} %param.26) | copy-start | bytes 393220
  6.5 168.1 %copy-start.2 = (bf16[8192,1,64]{0,2,1:T(8,128)(2,1)S(1)}, bf16[8192,1,64]{0,2,1:T(8,128)(2,1)}, u32[]{:S(2)}) copy-start(bf16[8192,1,64]{0,2,1:T(8,128)(2,1)} %param.19) | copy-start | bytes 3145732
  6.5 219.9 %all-gather.7.cloned.1.call-start = ((), (), s32[]{:S(2)}) async-start(), calls=%async_computation.3 | async-start | bytes 2359296 | tf_op jit(solution)/shard_map/all_gather | solution.py:14
  79.7 173.3 %reduce-scatter.2.cloned.1.call-start = ((), (), s32[]{:S(2)}) async-start(), calls=%async_computation.1 | async-start | bytes 98304 | tf_op jit(solution)/shard_map/reduce_scatter | solution.py:143
  215.1 29.3 %copy-start.6 = (f32[8192]{0:T(1024)S(1)}, f32[8192]{0:T(1024)}, u32[]{:S(2)}) copy-start(f32[8192]{0:T(1024)} %param.21) | copy-start | bytes 98308
  215.1 37.9 %copy-start.5 = (bf16[16,1,512]{2,0,1:T(8,128)(2,1)S(1)}, bf16[16,1,512]{2,0,1:T(8,128)(2,1)}, u32[]{:S(2)}) copy-start(bf16[16,1,512]{2,0,1:T(8,128)(2,1)} %param.15) | copy-start | bytes 49156
  244.4 78.0 %all-reduce.6.cloned.1.call-start = ((), (), s32[]{:S(2)}) async-start(), calls=%async_computation.4 | async-start | bytes 458752 | tf_op jit(solution)/shard_map/psum | solution.py:157
  295.2 109.0 %copy-start.1 = (bf16[8192,1,64]{0,2,1:T(8,128)(2,1)S(1)}, bf16[8192,1,64]{0,2,1:T(8,128)(2,1)}, u32[]{:S(2)}) copy-start(bf16[8192,1,64]{0,2,1:T(8,128)(2,1)} %param.18) | copy-start | bytes 3145732
  303.2 99.6 %all-reduce.4.cloned.1.call-start = ((), (), s32[]{:S(2)}) async-start(), calls=%async_computation.2 | async-start | bytes 524288 | tf_op jit(solution)/shard_map/psum | solution.py:162
Sparse Core Ops, SparseCore 0:
  79.8 53.2 all-gather.6
  244.5 8.4 reduce-scatter.1
  303.3 19.0 all-reduce.5
  330.5 72.2 all-reduce.3
where the time goes:
time: 412 us; the launch traced here: 411 us
  blocking collectives  223 us (54%)
  waiting for transfers between devices  100 us (24%)
  matrix products  37.1 us (9%)
  local copies, waits for them, and re-layouts  24.6 us (6%)
  between operations  13.3 us (3%)
  other arithmetic  12.6 us (3%)
    psum x1, waiting for transfers between devices, per_device(): down_total = lax.psum(down_part, 'tp')  72.4 us
    all_gather x2, blocking collectives, joined(): gathered = jax.tree.map(lambda a: lax.all_gather(a, axis), part)  62.7 us
    all_gather x1, blocking collectives, spread_rows(): across = lax.all_gather(shard, 'tp', axis=2, tiled=True)  32.7 us
    all_gather x1, blocking collectives, half_rows_of(): return lax.all_gather(shard, 'tp', axis=2, tiled=True)  30.8 us
    all_gather x1, blocking collectives, per_device(): lax.all_gather(key_part, 'tp', axis=1, tiled=True)  30.6 us
    all_gather x1, blocking collectives, per_device(): lax.all_gather(value_part, 'tp', axis=1, tiled=True)  30.6 us
    all_gather x1, blocking collectives, per_device(): lax.all_gather(query_part, 'tp', axis=1, tiled=True)  30.5 us
    psum x1, waiting for transfers between devices, per_device(): gate_total, up_total = lax.psum((gate_part, up_part), 'sub')  19.1 us
  transfers between devices with their start and end apart: 4, of which 3 were waited for; matrix products, arithmetic and copies ran while one was open for 6% of the time, Pallas kernels for 0%

commit v1 on v0

--- a/solution.py
+++ b/solution.py
@@ -159,7 +159,7 @@
     down_part = jnp.dot(
         hidden, w_down.reshape(hidden.shape[1], -1), preferred_element_type=jnp.float32
     )
-    down_total = lax.psum(down_part, "tp")
+    down_total = jnp.sum(lax.all_gather(down_part, "tp"), axis=0)
     down_share = lax.dynamic_slice_in_dim(down_total, tp_pos * shard_width, shard_width, 1)
     return (middle_float + down_share[:, None, :]).astype(jnp.bfloat16)
 

time: 412 us -> 391 us (0.949)
  waiting for transfers between devices: 100 us -> 78.2 us
    psum x1 -> x0, waiting for transfers between devices: 72.4 us -> none  [per_device(): down_total = lax.psum(down_part, 'tp')]
    all_gather x0 -> x1, waiting for transfers between devices: none -> 50.5 us  [per_device(): down_total = jnp.sum(lax.all_gather(down_part, 'tp'), axis=0)]
where the time goes in v1:
time: 391 us; the launch traced here: 390 us
  blocking collectives  223 us (57%)
  waiting for transfers between devices  78.2 us (20%)
  matrix products  37.2 us (10%)
  local copies, waits for them, and re-layouts  24.6 us (6%)
  other arithmetic  13.5 us (3%)
  between operations  13.4 us (3%)
    all_gather x2, blocking collectives, joined(): gathered = jax.tree.map(lambda a: lax.all_gather(a, axis), part)  62.7 us
    all_gather x1, waiting for transfers between devices, per_device(): down_total = jnp.sum(lax.all_gather(down_part, 'tp'), axis=0)  50.5 us
    all_gather x1, blocking collectives, spread_rows(): across = lax.all_gather(shard, 'tp', axis=2, tiled=True)  32.7 us
    all_gather x1, blocking collectives, half_rows_of(): return lax.all_gather(shard, 'tp', axis=2, tiled=True)  30.8 us
    all_gather x1, blocking collectives, per_device(): lax.all_gather(key_part, 'tp', axis=1, tiled=True)  30.6 us
    all_gather x1, blocking collectives, per_device(): lax.all_gather(value_part, 'tp', axis=1, tiled=True)  30.6 us
    all_gather x1, blocking collectives, per_device(): lax.all_gather(query_part, 'tp', axis=1, tiled=True)  30.5 us
    psum x1, waiting for transfers between devices, per_device(): gate_total, up_total = lax.psum((gate_part, up_part), 'sub')  19.1 us
  transfers between devices with their start and end apart: 4, of which 3 were waited for; matrix products, arithmetic and copies ran while one was open for 6% of the time, Pallas kernels for 0%

profile of v1, /device:TPU:0, one launch (start us, length us, event | category | flops | bytes accessed | tf_op | source)
XLA Modules:
  0.0 389.9 jit_solution(7088242958804928806)
XLA Ops:
  6.6 32.7 %all_gather.42 = bf16[16,1,4096]{2,0,1:T(8,128)(2,1)S(1)} all-gather(bf16[16,1,512]{2,0,1:T(8,128)(2,1)} %param.15), channel_id=1, replica_groups=mesh['grp'=2,'tp'=8,'sub'=2] {'tp'}, dimensions={2}, use_global_device_ids=true | all-gather | bytes 147456 | tf_op jit(solution)/shard_map/all_gather | solution.py:39
  39.2 2.0 all_gather.43
  42.4 4.7 %fusion.12 = bf16[16,512]{1,0:T(8,128)(2,1)S(1)} fusion(bf16[16,8192]{1,0:T(8,128)(2,1)S(1)} %bitcast.91, bf16[8192,1,512]{2,0,1:T(8,128)(2,1)} %param.17), kind=kOutput, calls=%fused_computation.18 | convolution fusion | flops 134225920 | bytes 8667136 | tf_op jit(solution)/shard_map/dot_general | solution.py:85
  47.1 30.5 %all_gather.44 = bf16[16,4096]{1,0:T(8,128)(2,1)S(1)} all-gather(bf16[16,512]{1,0:T(8,128)(2,1)S(1)} %fusion.12), channel_id=1, replica_groups=mesh['grp'=2,'tp'=8,'sub'=2] {'tp'}, dimensions={1}, use_global_device_ids=true | all-gather | bytes 147456 | tf_op jit(solution)/shard_map/all_gather | solution.py:95
  78.4 1.3 fusion.26
  80.0 31.0 %all-gather.1 = f32[128,4,8]{2,1,0:T(4,128)S(1)} all-gather(f32[16,4,8]{2,1,0:T(4,128)S(1)} %fusion.27), channel_id=3, replica_groups=mesh['grp'=2,'tp'=8,'sub'=2] {'tp'}, dimensions={0}, use_global_device_ids=true | all-gather | bytes 18432 | tf_op jit(solution)/shard_map/all_gather | solution.py:14
  111.2 31.7 %all-gather = f32[128,4,8]{2,1,0:T(4,128)S(1)} all-gather(f32[16,4,8]{2,1,0:T(4,128)S(1)} %get-tuple-element.236), channel_id=2, replica_groups=mesh['grp'=2,'tp'=8,'sub'=2] {'tp'}, dimensions={0}, use_global_device_ids=true | all-gather | bytes 18432 | tf_op jit(solution)/shard_map/all_gather | solution.py:14
  143.5 30.6 %all-gather.4 = bf16[8,64,16]{1,2,0:T(8,128)(2,1)S(1)} all-gather(bf16[1,64,16]{1,2,0:T(8,128)(2,1)S(1)} %fusion.15), channel_id=1, replica_groups=mesh['grp'=2,'tp'=8,'sub'=2] {'tp'}, dimensions={0}, use_global_device_ids=true | all-gather | bytes 18432 | tf_op jit(solution)/shard_map/all_gather | solution.py:96
  175.2 30.6 %all-gather.5 = bf16[8,64,16]{1,2,0:T(8,128)(2,1)S(1)} all-gather(bf16[1,64,16]{1,2,0:T(8,128)(2,1)S(1)} %fusion.16), channel_id=1, replica_groups=mesh['grp'=2,'tp'=8,'sub'=2] {'tp'}, dimensions={0}, use_global_device_ids=true | all-gather | bytes 18432 | tf_op jit(solution)/shard_map/all_gather | solution.py:97
  205.9 9.3 %copy.83 = bf16[512,8,2,512]{3,1,2,0:T(8,128)(2,1)} copy(bf16[512,8,2,512]{3,2,1,0:T(2,128)(2,1)} %bitcast.90) | data formatting | bytes 16777216
  215.2 11.4 %copy.75 = bf16[1024,4096]{1,0:T(8,128)(2,1)} copy(bf16[1024,4096]{0,1:T(8,128)(2,1)} %bitcast.89) | data formatting | bytes 16777216 | tf_op jit(solution)/shard_map/dot_general | solution.py:139
  227.6 10.0 %while.19 = (s32[]{:T(128)}, f32[16,4,8]{0,2,1:T(8,128)S(1)}, f32[16,4,8]{0,2,1:T(8,128)S(1)}, f32[16,4,8,128]{3,2,1,0:T(8,128)S(1)}, f32[8,16,4,8]{1,3,2,0:T(8,...) while((s32[]{:T(128)}, f32[16,4,8]{0,2,1:T(8,128)S(1)}, ...), condition=%wide.region_4.5_spmd, body=%wide.region_3.4_spmd.sunk | while | flops 199685 | bytes 815255 | solution.py:19
  230.6 1.2 fusion.58
  232.0 1.2 fusion.58
  238.2 6.3 %fusion.49 = f32[16,2,512]{2,0,1:T(8,128)} fusion(bf16[16,4096,1]{1,0,2:T(8,128)(2,1)S(1)} %reshape.199, bf16[2,512,4096]{2,1,0:T(8,128)(2,1)} %bitcast.88), kind=kOutput, calls=%fused_computation.77 | convolution fusion | flops 134217728 | bytes 8585216 | tf_op jit(solution)/shard_map/dot_general | solution.py:139
  244.6 8.6 %reduce-scatter.2.cloned.1.call-done = f32[16,1,512]{2,0,1:T(8,128)} async-done(((f32[16,2,512]{2,0,1:T(8,128)}), f32[16,1,512]{2,0,1:T(8,128)}) %reduce-scatter.2.cloned.1.call-update) | async-done | bytes 32784 | tf_op jit(solution)/shard_map/reduce_scatter | solution.py:143
  253.9 30.8 %all_gather.53 = bf16[16,1,4096]{2,0,1:T(8,128)(2,1)S(1)} all-gather(bf16[16,1,512]{2,0,1:T(8,128)(2,1)S(1)} %add_convert_fusion.1), channel_id=1, replica_groups=mesh['grp'=2,'tp'=8,'sub'=2] {'tp'}, dimensions={2}, use_global_device_ids=true | all-gather | bytes 147456 | tf_op jit(solution)/shard_map/all_gather | solution.py:44
  284.8 2.6 psum.21
  287.5 7.9 %fusion.7 = f32[16,1792]{1,0:T(8,128)} fusion(bf16[1,4096,1792]{2,1,0:T(8,128)(2,1)} %param.22, bf16[16,1,4096]{2,0,1:T(8,128)(2,1)S(1)} %all_gather.53, f32[4096]{0:T(1024)S(1)} %dynamic_slice.50, f32[16]{0:T(128)S(1)} %add_rsqrt_fusion), kind=kOutput, calls=%fused_computation.12 | convolution fusion | flops 235143168 | bytes 14942272 | tf_op jit(solution)/shard_map/dot_general | solution.py:153
  295.3 7.9 %fusion.5 = f32[16,1792]{1,0:T(8,128)} fusion(bf16[1,4096,1792]{2,1,0:T(8,128)(2,1)} %param.23, bf16[16,1,4096]{2,0,1:T(8,128)(2,1)S(1)} %all_gather.53, f32[4096]{0:T(1024)S(1)} %dynamic_slice.50, f32[16]{0:T(128)S(1)} %add_rsqrt_fusion), kind=kOutput, calls=%fused_computation.10 | convolution fusion | flops 235143168 | bytes 14942272 | tf_op jit(solution)/shard_map/dot_general | solution.py:156
  303.3 19.1 %all-reduce.3.cloned.1.call-done = (f32[16,1792]{1,0:T(8,128)}, f32[16,1792]{1,0:T(8,128)}) async-done(((f32[16,1792]{1,0:T(8,128)}, f32[16,1792]{1,0:T(8,128)}), (f32[16,1792]{1,0:T(8,128)}, f32[16,1792]{1,0:T(8,128)})) %all-reduce.3.cloned.1.call-update) | async-done | bytes 229392 | tf_op jit(solution)/shard_map/psum | solution.py:157
  322.4 8.1 %fusion.3 = f32[16,4096]{1,0:T(8,128)} fusion(bf16[1792,1,4096]{2,0,1:T(8,128)(2,1)} %param.24, f32[16,1792]{1,0:T(8,128)} %get-tuple-element.221, f32[16,1792]{1,0:T(8,128)} %get-tuple-element.222), kind=kOutput, calls=%fused_computation.8 | convolution fusion | flops 235053056 | bytes 15171584 | tf_op jit(solution)/shard_map/dot_general | solution.py:159
  330.6 50.5 %all-gather.11.cloned.1.call-done = f32[128,4096]{1,0:T(8,128)} async-done(((f32[16,4096]{1,0:T(8,128)}), f32[128,4096]{1,0:T(8,128)}) %all-gather.11.cloned.1.call-update) | async-done | bytes 2097168 | tf_op jit(solution)/shard_map/all_gather | solution.py:162
  381.0 1.7 reduce_sum.49
  (96 shorter events, 14.6 us)
Async XLA Ops:
  6.5 136.6 %copy-start = (bf16[8192,1,64]{0,2,1:T(8,128)(2,1)S(1)}, bf16[8192,1,64]{0,2,1:T(8,128)(2,1)}, u32[]{:S(2)}) copy-start(bf16[8192,1,64]{0,2,1:T(8,128)(2,1)} %param.18) | copy-start | bytes 3145732
  6.5 220.0 %all-gather.9.cloned.1.call-start = ((), (), s32[]{:S(2)}) async-start(), calls=%async_computation.2 | async-start | bytes 2359296 | tf_op jit(solution)/shard_map/all_gather | solution.py:14
  42.4 35.3 %copy-start.7 = (s32[16]{0:T(128)S(1)}, s32[16]{0:T(128)}, u32[]{:S(2)}) copy-start(s32[16]{0:T(128)} %param.27) | copy-start | bytes 196
  42.4 35.7 %copy-start.3 = (bf16[16,8,4,128]{3,2,1,0:T(4,128)(2,1)S(1)}, bf16[16,8,4,128]{3,2,1,0:T(4,128)(2,1)}, u32[]{:S(2)}) copy-start(bf16[16,8,4,128]{3,2,1,0:T(4,128)(2,1)} %param.25) | copy-start | bytes 393220
  42.4 36.0 %copy-start.4 = (bf16[16,8,4,128]{3,2,1,0:T(4,128)(2,1)S(1)}, bf16[16,8,4,128]{3,2,1,0:T(4,128)(2,1)}, u32[]{:S(2)}) copy-start(bf16[16,8,4,128]{3,2,1,0:T(4,128)(2,1)} %param.26) | copy-start | bytes 393220
  42.4 132.4 %copy-start.2 = (bf16[8192,1,64]{0,2,1:T(8,128)(2,1)S(1)}, bf16[8192,1,64]{0,2,1:T(8,128)(2,1)}, u32[]{:S(2)}) copy-start(bf16[8192,1,64]{0,2,1:T(8,128)(2,1)} %param.19) | copy-start | bytes 3145732
  79.8 173.4 %reduce-scatter.2.cloned.1.call-start = ((), (), s32[]{:S(2)}) async-start(), calls=%async_computation.1 | async-start | bytes 98304 | tf_op jit(solution)/shard_map/reduce_scatter | solution.py:143
  226.6 18.0 %copy-start.6 = (f32[8192]{0:T(1024)S(1)}, f32[8192]{0:T(1024)}, u32[]{:S(2)}) copy-start(f32[8192]{0:T(1024)} %param.21) | copy-start | bytes 98308
  226.6 26.6 %copy-start.5 = (bf16[16,1,512]{2,0,1:T(8,128)(2,1)S(1)}, bf16[16,1,512]{2,0,1:T(8,128)(2,1)}, u32[]{:S(2)}) copy-start(bf16[16,1,512]{2,0,1:T(8,128)(2,1)} %param.15) | copy-start | bytes 49156
  244.5 77.9 %all-reduce.3.cloned.1.call-start = ((), (), s32[]{:S(2)}) async-start(), calls=%async_computation.4 | async-start | bytes 458752 | tf_op jit(solution)/shard_map/psum | solution.py:157
  303.2 77.8 %all-gather.11.cloned.1.call-start = ((), (), s32[]{:S(2)}) async-start(), calls=%async_computation.3 | async-start | bytes 2359296 | tf_op jit(solution)/shard_map/all_gather | solution.py:162
  322.4 60.9 %copy-start.1 = (bf16[8192,1,64]{0,2,1:T(8,128)(2,1)S(1)}, bf16[8192,1,64]{0,2,1:T(8,128)(2,1)}, u32[]{:S(2)}) copy-start(bf16[8192,1,64]{0,2,1:T(8,128)(2,1)} %param.18) | copy-start | bytes 3145732
Sparse Core Ops, SparseCore 0:
  79.9 53.2 all-gather.8
  244.6 8.4 reduce-scatter.1
  303.4 19.0 all-reduce.2
  330.7 50.2 all-gather.10
